TPU v7x, 32 devices: a whole 2x2x4 slice. The times are simulated.
32 devices in a mesh: gz: 32 (over z, y, x, core).
Axes of the slice: x: 2, y: 2, z: 4, core: 2. Of those that a mesh axis runs over, the one named last changes fastest.
Arguments:
- velocity: float32 [3, 128, 256, 512], P(None, 'gz'), may hold values from -0.3 to 0.3
- offsets: float32 [3, 16384], P(None, 'gz'), may hold values from 1.2 to 1.8
- bases: int32 [3, 16384], P(None, 'gz'), may hold values from 0 to 511, as said below
- targets: float32 [3, 16384], P(None, 'gz'), may hold values from 1 to 2
- stiffness: float32 [16384], P('gz'), may hold values from 10 to 100
- active_block_count: int32 [32], P('gz'), may hold values from 1 to 2, as said below
Outputs:
- velocity_out: float32 [3, 128, 256, 512], P(None, 'gz')
- offsets_out: float32 [3, 16384], P(None, 'gz')
Inputs may be any that keep to these rules, and one draw needn't show every extreme that they name: `bases`: rows are x, y, z. x lies in 0..511 and y in 0..255; the z of marker m lies in the slab of index m // 512, from (m // 512) * 4 to (m // 512) * 4 + 3. `active_block_count`: in every draw some slab uses all 2 blocks.
All inputs are finite; a program needn't handle non-finite values.
Results may differ from a plain program's by a relative error of at most 0.0015.
Values may be sent and summed in bfloat16 or wider, within the bound.
A program may use at most 192 MiB of HBM per device.

v0:
```python
import functools
import math

import jax
import jax.numpy as jnp
from jax import lax
from jax.experimental import pallas as pl
from jax.experimental.pallas import tpu as pltpu
from jax.sharding import PartitionSpec as P

BLK = 256
STEPS = 2
DT = 0.2
VISC = 0.3
TABLE = 128
ROWS = 16


def shifted(value, steps):
    count = lax.axis_size("gz")
    pairs = [(source, (source + steps) % count) for source in range(count)]
    return lax.ppermute(value, "gz", pairs)


def joined(own_ref, near_ref, moved, layers):
    halves = []
    for ref, pair in ((own_ref, moved[:2]), (near_ref, moved[2:])):
        rows = ref[...]
        offsets = rows[0:3]
        if pair:
            sampled = pair[0][0:3, :] + pair[1][0:3, :]
            offsets = offsets + DT * (rows[9:10] * sampled)
        level = rows[5:6] if ref is own_ref else rows[5:6] - float(layers)
        forces = rows[10:11] * (rows[6:9] - offsets)
        halves.append((offsets, rows[3:5].astype(jnp.int32), level.astype(jnp.int32), forces))
    return [jnp.concatenate(parts, axis=1) for parts in zip(*halves)]


def weights_of(offsets):
    angle = (0.5 * math.pi) * offsets
    c, s = jnp.cos(angle), jnp.sin(angle)
    return [0.25 * (1.0 + c), 0.25 * (1.0 + s), 0.25 * (1.0 - c), 0.25 * (1.0 - s)]


def banded(across, cell, weights, extent):
    apart = across - cell
    if extent & (extent - 1) == 0:
        apart = apart & (extent - 1)
    else:
        apart = jnp.where(apart < 0, apart + extent, apart)
    table = jnp.where(apart == 3, weights[3], 0.0)
    for j in (2, 1, 0):
        table = jnp.where(apart == j, weights[j], table)
    return table


def plane_weights(level, weights_z, layers):
    planes = []
    for z in range(layers):
        row = jnp.zeros(level.shape, jnp.float32)
        for j in range(4):
            row = jnp.where(level + j == z, weights_z[j], row)
        planes.append(row)
    return planes


def columns_of(rows):
    pad = -len(rows) % 8
    zero = jnp.zeros_like(rows[0])
    return jnp.concatenate(rows + [zero] * pad, axis=0).T


def fill_xtable(table_ref, col_ref, first, low, extent, chunk):
    def body(i, _):
        r = pl.ds(i * chunk, chunk)
        cols = col_ref[r, :]
        across = lax.broadcasted_iota(jnp.int32, (chunk, extent), 1)
        cell = cols[:, first : first + 1].astype(jnp.int32)
        ws = [cols[:, first + 1 + j : first + 2 + j] for j in range(4)]
        table_ref[r, :] = banded(across, cell, ws, extent).astype(low)
        return 0

    lax.fori_loop(0, table_ref.shape[0] // chunk, body, 0)


def stencil_kernel(v_hbm, p_hbm, vbuf, obuf, in_sem, out_sem):
    layers, ny, nx = vbuf.shape[1:]

    def load(z):
        return pltpu.make_async_copy(v_hbm.at[:, z], vbuf.at[:, z], in_sem.at[z])

    def store(z):
        return pltpu.make_async_copy(obuf.at[:, z], p_hbm.at[:, z], out_sem.at[z])

    for z in range(layers):
        load(z).start()
    load(0).wait()

    def plane(z, _):
        @pl.when(z < layers - 1)
        def _():
            load(z + 1).wait()

        below = jnp.maximum(z - 1, 0)
        above = jnp.minimum(z + 1, layers - 1)
        has_below = jnp.where(z > 0, 1.0, 0.0)
        has_above = jnp.where(z < layers - 1, 1.0, 0.0)

        def stencil(i, _):
            n = 8
            y0 = i * n
            prev = jnp.where(i == 0, ny - 8, y0 - 8)
            nxt = jnp.where(y0 + n == ny, 0, y0 + n)
            here = [vbuf[c, z, pl.ds(y0, n), :] for c in range(3)]
            up = [DT * VISC - (0.5 * DT) * here[c] for c in range(3)]
            down = [DT * VISC + (0.5 * DT) * here[c] for c in range(3)]
            up[2] = up[2] * has_above
            down[2] = down[2] * has_below
            for c in range(3):
                window = jnp.concatenate(
                    [vbuf[c, z, pl.ds(prev, 8), :], here[c], vbuf[c, z, pl.ds(nxt, 8), :]], axis=0
                )
                total = (1.0 - 6.0 * DT * VISC) * here[c]
                total += up[0] * pltpu.roll(here[c], nx - 1, 1) + down[0] * pltpu.roll(here[c], 1, 1)
                total += up[1] * pltpu.roll(window, n + 15, 0)[8 : 8 + n]
                total += down[1] * pltpu.roll(window, 1, 0)[8 : 8 + n]
                total += up[2] * vbuf[c, above, pl.ds(y0, n), :]
                total += down[2] * vbuf[c, below, pl.ds(y0, n), :]
                obuf[c, z, pl.ds(y0, n), :] = total
            return 0

        lax.fori_loop(0, ny // 8, stencil, 0, unroll=2)
        store(z).start()
        return 0

    lax.fori_loop(0, layers, plane, 0)
    for z in range(layers):
        store(z).wait()


def stencil_terms(velocity):
    layers = velocity.shape[1]
    hbm = pl.BlockSpec(memory_space=pl.ANY)
    return pl.pallas_call(
        stencil_kernel,
        out_shape=jax.ShapeDtypeStruct(velocity.shape, jnp.float32),
        in_specs=[hbm],
        out_specs=hbm,
        scratch_shapes=[
            pltpu.VMEM(velocity.shape, jnp.float32),
            pltpu.VMEM(velocity.shape, jnp.float32),
            pltpu.SemaphoreType.DMA((layers,)),
            pltpu.SemaphoreType.DMA((layers,)),
        ],
        cost_estimate=pl.CostEstimate(
            flops=6000 * velocity.size, bytes_accessed=8 * velocity.size, transcendentals=0
        ),
        name="stencil_terms",
    )(velocity)


def spread_kernel(layers, n_moved, *refs):
    own_ref, near_ref = refs[:2]
    moved = refs[2 : 2 + n_moved]
    v_hbm, p_hbm, col = refs[2 + n_moved : 5 + n_moved]
    obuf, force, lhs, xtab, ytab, rowg, in_sem, out_sem = refs[5 + n_moved :]
    ny, nx = obuf.shape[2], obuf.shape[3]
    both = xtab.shape[0]

    load = pltpu.make_async_copy(v_hbm, obuf, in_sem)
    load.start()

    offsets, cells, level, forces = joined(own_ref, near_ref, moved, layers)
    weights = weights_of(offsets)
    planes = plane_weights(level, [w[2:3] for w in weights], layers)
    rows = []
    for a in range(2):
        rows += [cells[a : a + 1].astype(jnp.float32)] + [w[a : a + 1] for w in weights]
    col[...] = columns_of(rows + planes)
    for z in range(layers):
        rowg[z] = jnp.concatenate([forces * planes[z], jnp.zeros((5, both), jnp.float32)], axis=0)
    fill_xtable(xtab, col, 0, jnp.bfloat16, nx, TABLE)

    wy = [w[1:2] for w in weights]

    def ybody(i, _):
        across = lax.broadcasted_iota(jnp.int32, (32, both), 0) + i * 32
        ytab[pl.ds(i * 32, 32), :] = banded(across, cells[1:2], wy, ny)
        return 0

    lax.fori_loop(0, ny // 32, ybody, 0)
    load.wait()

    def plane(z, _):
        def lhs_body(i, _):
            y = ytab[pl.ds(i * 16, 16), :]
            for c in range(3):
                lhs[pl.ds(c * ny + i * 16, 16), :] = (rowg[z, c : c + 1, :] * y).astype(jnp.bfloat16)
            return 0

        lax.fori_loop(0, ny // 16, lhs_body, 0)
        force[...] = jnp.dot(lhs[...], xtab[...], preferred_element_type=jnp.float32)

        def add(i, _):
            r = pl.ds(i * 32, 32)
            for c in range(3):
                obuf[c, z, r, :] += DT * force[pl.ds(c * ny + i * 32, 32), :]
            return 0

        lax.fori_loop(0, ny // 32, add, 0)
        pltpu.make_async_copy(obuf.at[:, z], p_hbm.at[:, z], out_sem.at[z]).start()
        return 0

    lax.fori_loop(0, layers, plane, 0)
    for z in range(layers):
        pltpu.make_async_copy(obuf.at[:, z], p_hbm.at[:, z], out_sem.at[z]).wait()


def add_forcing(own, near, moved, velocity):
    _, layers, ny, nx = velocity.shape
    both = 2 * own.shape[1]
    vmem = pl.BlockSpec(memory_space=pltpu.VMEM)
    hbm = pl.BlockSpec(memory_space=pl.ANY)
    flops = 2 * both * 3 * layers * ny * nx
    return pl.pallas_call(
        functools.partial(spread_kernel, layers, len(moved)),
        out_shape=[
            jax.ShapeDtypeStruct(velocity.shape, jnp.float32),
            jax.ShapeDtypeStruct((both, 16), jnp.float32),
        ],
        in_specs=[vmem] * (2 + len(moved)) + [hbm],
        out_specs=[hbm, vmem],
        input_output_aliases={2 + len(moved): 0},
        scratch_shapes=[
            pltpu.VMEM(velocity.shape, jnp.float32),
            pltpu.VMEM((3 * ny, nx), jnp.float32),
            pltpu.VMEM((3 * ny, both), jnp.bfloat16),
            pltpu.VMEM((both, nx), jnp.bfloat16),
            pltpu.VMEM((ny, both), jnp.float32),
            pltpu.VMEM((layers, 8, both), jnp.float32),
            pltpu.SemaphoreType.DMA,
            pltpu.SemaphoreType.DMA((layers,)),
        ],
        cost_estimate=pl.CostEstimate(
            flops=flops, bytes_accessed=8 * velocity.size, transcendentals=0
        ),
        name="add_forcing",
    )(own, near, *moved, velocity)


def sample_kernel(layers, send, *refs):
    col, v_hbm, p_hbm, before_hbm, after_hbm, out_hbm, own_out, near_out = refs[:8]
    low_hbm = refs[8 : 8 + 2 * send]
    vbuf, vz, halo, low, lhs, xtab, sem, out_sem = refs[8 + 2 * send :]
    ny, nx = vbuf.shape[2], vbuf.shape[3]
    both = xtab.shape[0]
    markers = both // 2
    edges = ((0, before_hbm, 0.5 * DT), (layers - 1, after_hbm, -0.5 * DT))

    loads = []
    for side, (z, halo_hbm, _) in enumerate(edges):
        loads.append(pltpu.make_async_copy(p_hbm.at[:, z], vbuf.at[:, z], sem.at[z]))
        loads.append(pltpu.make_async_copy(v_hbm.at[2, z], vz.at[side], sem.at[layers + side]))
        loads.append(pltpu.make_async_copy(halo_hbm, halo.at[side], sem.at[layers + 2 + side]))
    for z in range(1, layers - 1):
        loads.append(pltpu.make_async_copy(p_hbm.at[:, z], vbuf.at[:, z], sem.at[z]))
    for load in loads:
        load.start()

    fill_xtable(xtab, col, 0, jnp.float32, nx, TABLE)

    def lhs_body(i, _):
        r = pl.ds(i * TABLE, TABLE)
        cols = col[r, :]
        across = lax.broadcasted_iota(jnp.int32, (TABLE, ny), 1)
        cell = cols[:, 5:6].astype(jnp.int32)
        y = banded(across, cell, [cols[:, 6 + j : 7 + j] for j in range(4)], ny)
        for z in range(layers):
            lhs[r, z * ny : (z + 1) * ny] = (cols[:, 10 + z : 11 + z] * y).astype(jnp.bfloat16)
        return 0

    lax.fori_loop(0, both // TABLE, lhs_body, 0)
    for load in loads:
        load.wait()

    stores = []
    for side, (z, _, sign) in enumerate(edges):

        def edge_body(i, _):
            r = pl.ds(i * 32, 32)
            factor = DT * VISC + sign * vz[side, r, :]
            for c in range(3):
                new = vbuf[c, z, r, :] + factor * halo[side, c, r, :].astype(jnp.float32)
                vbuf[c, z, r, :] = new
                low[c, pl.ds(z * ny + i * 32, 32), :] = new.astype(jnp.bfloat16)
            return 0

        lax.fori_loop(0, ny // 32, edge_body, 0)
        stores.append(pltpu.make_async_copy(vbuf.at[:, z], out_hbm.at[:, z], out_sem.at[side]))
        if send:
            stores.append(
                pltpu.make_async_copy(
                    low.at[:, z * ny : (z + 1) * ny], low_hbm[side], out_sem.at[2 + side]
                )
            )
    for store in stores:
        store.start()

    def low_body(i, _):
        r = pl.ds(i * 32, 32)
        for z in range(1, layers - 1):
            for c in range(3):
                low[c, pl.ds(z * ny + i * 32, 32), :] = vbuf[c, z, r, :].astype(jnp.bfloat16)
        return 0

    lax.fori_loop(0, ny // 32, low_body, 0)

    for part, out, depth in ((0, own_out, layers * ny), (1, near_out, 3 * ny)):
        r = slice(part * markers, (part + 1) * markers)
        sums = []
        for c in range(3):
            lines = jnp.dot(
                lhs[r, :depth], low[c, :depth, :], preferred_element_type=jnp.float32
            )
            sums.append(jnp.sum(lines * xtab[r, :], axis=1, keepdims=True))
        zero = jnp.zeros((markers, 5), jnp.float32)
        out[...] = jnp.concatenate(sums + [zero], axis=1).T
    for store in stores:
        store.wait()


def finish_and_sample(col, velocity, partial, before, after, send):
    _, layers, ny, nx = velocity.shape
    both = col.shape[0]
    markers = both // 2
    vmem = pl.BlockSpec(memory_space=pltpu.VMEM)
    hbm = pl.BlockSpec(memory_space=pl.ANY)
    part = jax.ShapeDtypeStruct((8, markers), jnp.float32)
    low = jax.ShapeDtypeStruct((3, ny, nx), jnp.bfloat16)
    return pl.pallas_call(
        functools.partial(sample_kernel, layers, send),
        out_shape=[jax.ShapeDtypeStruct(velocity.shape, jnp.float32), part, part] + [low, low] * send,
        in_specs=[vmem] + [hbm] * 4,
        out_specs=[hbm, vmem, vmem] + [hbm, hbm] * send,
        input_output_aliases={2: 0},
        scratch_shapes=[
            pltpu.VMEM(velocity.shape, jnp.float32),
            pltpu.VMEM((2, ny, nx), jnp.float32),
            pltpu.VMEM((2, 3, ny, nx), jnp.bfloat16),
            pltpu.VMEM((3, layers * ny, nx), jnp.bfloat16),
            pltpu.VMEM((both, layers * ny), jnp.bfloat16),
            pltpu.VMEM((both, nx), jnp.float32),
            pltpu.SemaphoreType.DMA((layers + 4,)),
            pltpu.SemaphoreType.DMA((4,)),
        ],
        cost_estimate=pl.CostEstimate(
            flops=2 * both * 3 * layers * ny * nx,
            bytes_accessed=4 * velocity.size,
            transcendentals=0,
        ),
        name="finish_and_sample",
    )(col, velocity, partial, before, after)


def local(velocity, offsets, bases, targets, stiffness, active_block_count):
    layers = velocity.shape[1]
    markers = offsets.shape[1]
    living = (jnp.arange(markers, dtype=jnp.int32) // BLK < active_block_count[0]).astype(jnp.float32)
    level = bases[2] - lax.axis_index("gz") * layers
    own = jnp.concatenate(
        [
            offsets,
            bases[:2].astype(jnp.float32),
            level[None].astype(jnp.float32),
            targets,
            living[None],
            (living * stiffness)[None],
            jnp.zeros((ROWS - 11, markers), jnp.float32),
        ],
        axis=0,
    )
    first = velocity[:, 0].astype(jnp.bfloat16)
    final = velocity[:, layers - 1].astype(jnp.bfloat16)
    own, first, final = lax.optimization_barrier((own, first, final))
    near = shifted(own, 1)
    moved = ()
    for step in range(STEPS):
        last = step == STEPS - 1
        before = shifted(final, 1)
        after = shifted(first, -1)
        partial = stencil_terms(velocity)
        partial, col = add_forcing(own, near, moved, partial)
        velocity, own_part, near_part, *low = finish_and_sample(
            col, velocity, partial, before, after, 0 if last else 1
        )
        back = shifted(near_part, -1)
        if not last:
            first, final = low
            moved = (own_part, back, shifted(own_part, 1), near_part)
        offsets = offsets + DT * (living[None, :] * (own_part[:3] + back[:3]))
    return (velocity, offsets)


def solution(mesh):
    return jax.shard_map(
        local,
        mesh=mesh,
        in_specs=(
            P(None, "gz", None, None),
            P(None, "gz"),
            P(None, "gz"),
            P(None, "gz"),
            P("gz"),
            P("gz"),
        ),
        out_specs=(P(None, "gz", None, None), P(None, "gz")),
        check_vma=False,
    )
```

profile of v0, /device:TPU:1, one launch (start us, length us, event | category | flops | bytes accessed | tf_op | source)
XLA Modules:
  0.0 91.0 jit_solution(8760859931479075267)
XLA Ops:
  1.3 0.7 slice_convert_fusion
  2.0 0.7 subtract_convert_fusion
  2.7 2.1 %slice_bitcast_fusion = (bf16[3,256,512]{2,1,0:T(8,128)(2,1)S(1)}, bf16[3,256,512]{2,1,0:T(8,128)(2,1)S(1)}) fusion(f32[3,4,256,512]{3,2,1,0:T(8,128)} %refs_1_.1), kind=kLoop, calls=%fused_computation.1 | loop fusion | bytes 3145728 | tf_op jit(solution)/shard_map/convert_element_type | solution.py:383
  4.8 0.7 broadcast_select_fusion
  5.5 1.5 %concatenate.3.refs_0_ = f32[16,512]{1,0:T(8,128)S(1)} concatenate(f32[3,512]{1,0:T(4,128)} %param.7, f32[2,512]{1,0:T(2,128)S(1)} %slice_convert_fusion, f32[1,512]{1,0:T(1,128)S(1)} %subtract_convert_fusion, f32[3,512]{1,0:T(4,128)} %param.9, f32[1,512]{1,0:T(1,128)S(1)} %compare_convert_fusion, f32[1,512]{1,0:T(1,128)S(1)} %bitcast.9, f32[5,512]{1,0:T(8,128)S(1)} %broadcast_in_dim.5), dimensions={0} | concatenate | bytes 65536 | tf_op jit(solution)/shard_map/concatenate | solution.py:370
  7.0 2.6 %collective-permute-start = (f32[16,512]{1,0:T(8,128)S(1)}, f32[16,512]{1,0:T(8,128)S(1)}, u32[]{:S(2)}, u32[]{:S(2)}) collective-permute-start(f32[16,512]{1,0:T(8,128)S(1)} %concatenate.3.refs_0_), channel_id=1, source_target_pairs={{0,1},{1,2},{2,3},{3,4},{4,5},{5,6},{6,7},{7,8},{8,9},{9,10},{10,1... | collective-permute-start | bytes 98312 | tf_op jit(solution)/shard_map/ppermute | solution.py:22
  9.7 0.1 collective-permute-start.1
  9.7 0.4 collective-permute-start.2
  10.2 11.2 %stencil_terms.2.refs_2_ = f32[3,4,256,512]{3,2,1,0:T(8,128)} custom-call(f32[3,4,256,512]{3,2,1,0:T(8,128)} %refs_1_.1), custom_call_target="tpu_custom_call" | custom-call | flops 9437184000 | bytes 12582912 | tf_op jit(solution)/shard_map/stencil_terms/pallas_call | solution.py:144
  21.4 0.6 copy-done.9
  22.0 11.7 %add_forcing.2 = (f32[3,4,256,512]{3,2,1,0:T(8,128)}, f32[1024,16]{1,0:T(8,128)}) custom-call(f32[16,512]{1,0:T(8,128)} %copy-done.5, f32[16,512]{1,0:T(8,128)} %copy-done.9, f32[3,4,256,512]{3,2,1,0:T(8,128)} %stencil_terms.2.refs_2_), custom_call_target="tpu_custom_call", output_to_operand_aliasing={{0}: (2, {})} | custom-call | flops 3221225472 | bytes 12582912 | tf_op jit(solution)/shard_map/add_forcing/pallas_call | solution.py:225
  33.8 0.0 copy-start.2
  33.8 0.0 collective-permute-done.2.refs_4_
  33.8 0.8 copy-done.2
  34.7 0.3 copy-done.3
  35.0 9.2 %finish_and_sample.2 = (f32[3,4,256,512]{3,2,1,0:T(8,128)}, f32[8,512]{1,0:T(8,128)}, f32[8,512]{1,0:T(8,128)}, bf16[3,256,512]{2,1,0:T(8,128)(2,1)}, bf16[3,256,512]{2,1,0:T(8,128)(2,1)}) custom-call(f32[1024,16]{1,0:T(8,128)} %get-tuple-element.18.refs_0_, f32[3,4,256,512]{3,2,1,0:T(8,128)} %refs_1_.1, ...), custom_call_target="tpu_custom_call", output_to_operand_aliasing={{0}: (2, {})} | custom-call | flops 3221225472 | bytes 6291456 | tf_op jit(solution)/shard_map/finish_and_sample/pallas_call | solution.py:340
  44.3 3.5 %collective-permute-start.3 = (f32[8,512]{1,0:T(8,128)}, f32[8,512]{1,0:T(8,128)S(1)}, u32[]{:S(2)}, u32[]{:S(2)}) collective-permute-start(f32[8,512]{1,0:T(8,128)} %get-tuple-element.23.refs_5_), channel_id=1, source_target_pairs={{0,31},{1,0},{2,1},{3,2},{4,3},{5,4},{6,5},{7,6},{8,7},{9,8},{10,9... | collective-permute-start | bytes 49160 | tf_op jit(solution)/shard_map/ppermute | solution.py:22
  47.8 0.0 collective-permute-start.4
  47.8 0.0 collective-permute-start.5
  47.8 0.7 collective-permute-start.6
  48.5 11.2 %stencil_terms.3.refs_6_ = f32[3,4,256,512]{3,2,1,0:T(8,128)} custom-call(f32[3,4,256,512]{3,2,1,0:T(8,128)} %get-tuple-element.24.v_hbm.refs_1_), custom_call_target="tpu_custom_call" | custom-call | flops 9437184000 | bytes 12582912 | tf_op jit(solution)/shard_map/stencil_terms/pallas_call | solution.py:144
  59.7 0.0 collective-permute-done.3.refs_3_
  59.7 0.6 copy-done.7
  60.3 0.6 copy-done.10
  60.9 11.8 %add_forcing.3 = (f32[3,4,256,512]{3,2,1,0:T(8,128)}, f32[1024,16]{1,0:T(8,128)}) custom-call(f32[16,512]{1,0:T(8,128)} %copy-done.5, f32[16,512]{1,0:T(8,128)} %copy-done.9, f32[8,512]{1,0:T(8,128)} %get-tuple-element.22.refs_2_, f32[8,512]{1,0:T(8,128)} %copy-done.7, f32[8,512]{1,0:T(8,128)} %copy-done.10, ...), custom_call_target="tpu_custom_call", output_to_operand_aliasing={{0}: (6, {})} | custom-call | flops 3221225472 | bytes 12582912 | tf_op jit(solution)/shard_map/add_forcing/pallas_call | solution.py:225
  72.7 0.0 collective-permute-done.5.refs_3_
  72.7 0.9 copy-done
  73.6 0.3 copy-done.1
  73.9 9.3 %finish_and_sample.3 = (f32[3,4,256,512]{3,2,1,0:T(8,128)}, f32[8,512]{1,0:T(8,128)}, f32[8,512]{1,0:T(8,128)}) custom-call(f32[1024,16]{1,0:T(8,128)} %get-tuple-element.25.refs_0_, f32[3,4,256,512]{3,2,1,0:T(8,128)} %get-tuple-element.24.v_hbm.refs_1_, f32[3,4,256,512]{3,2,1,0:T(8,128)} %get-tuple-element.26.refs_2_, ...), custom_call_target="tpu_custom_call", output_to_operand_aliasing={{0}: (2, {})} | custom-call | flops 3221225472 | bytes 6291456 | tf_op jit(solution)/shard_map/finish_and_sample/pallas_call | solution.py:340
  83.2 5.4 %collective-permute-start.7 = (f32[8,512]{1,0:T(8,128)}, f32[8,512]{1,0:T(8,128)S(1)}, u32[]{:S(2)}, u32[]{:S(2)}) collective-permute-start(f32[8,512]{1,0:T(8,128)} %get-tuple-element.31), channel_id=1, source_target_pairs={{0,31},{1,0},{2,1},{3,2},{4,3},{5,4},{6,5},{7,6},{8,7},{9,8},{10,9... | collective-permute-start | bytes 49160 | tf_op jit(solution)/shard_map/ppermute | solution.py:22
  88.6 1.0 %collective-permute-done.7 = f32[8,512]{1,0:T(8,128)S(1)} collective-permute-done((f32[8,512]{1,0:T(8,128)}, f32[8,512]{1,0:T(8,128)S(1)}, u32[]{:S(2)}, u32[]{:S(2)}) %collective-permute-start.7) | collective-permute-done | bytes 16416 | tf_op jit(solution)/shard_map/ppermute | solution.py:22
  89.6 1.3 %fusion.2 = f32[3,512]{1,0:T(4,128)} fusion(f32[8,512]{1,0:T(8,128)S(1)} %collective-permute-done.7, f32[3,512]{1,0:T(4,128)S(1)} %copy-done.4, f32[8,512]{1,0:T(8,128)S(1)} %copy-done.8, f32[8,512]{1,0:T(8,128)} %get-tuple-element.30, f32[8,512]{1,0:T(8,128)S(1)} %copy-done.6, f32[512]{0:T(512)S(1)} %fusion.10), kind=kLoop, calls=%fused_computation.6 | loop fusion | flops 12288 | bytes 38912 | tf_op jit(solution)/shard_map/add | solution.py:400
  (21 shorter events, 0.1 us)
Async XLA Ops:
  7.0 14.4 %copy-start.5 = (f32[16,512]{1,0:T(8,128)}, f32[16,512]{1,0:T(8,128)S(1)}, u32[]{:S(2)}) copy-start(f32[16,512]{1,0:T(8,128)S(1)} %concatenate.3.refs_0_) | copy-start | bytes 98308
  7.0 14.4 %collective-permute-start = (f32[16,512]{1,0:T(8,128)S(1)}, f32[16,512]{1,0:T(8,128)S(1)}, u32[]{:S(2)}, u32[]{:S(2)}) collective-permute-start(f32[16,512]{1,0:T(8,128)S(1)} %concatenate.3.refs_0_), channel_id=1, source_target_pairs={{0,1},{1,2},{2,3},{3,4},{4,5},{5,6},{6,7},{7,8},{8,9},{9,10},{10,1... | collective-permute-start | bytes 98312 | tf_op jit(solution)/shard_map/ppermute | solution.py:22
  9.7 24.1 %collective-permute-start.1 = (bf16[3,256,512]{2,1,0:T(8,128)(2,1)S(1)}, bf16[3,256,512]{2,1,0:T(8,128)(2,1)S(1)}, u32[]{:S(2)}, u32[]{:S(2)}) collective-permute-start(bf16[3,256,512]{2,1,0:T(8,128)(2,1)S(1)} %get-tuple-element.20), channel_id=1, source_target_pairs={{0,1},{1,2},{2,3},{3,4},{4,5},{5,6},{6,7},{7,8},{8,9},{9,10},{10,1... | collective-permute-start | bytes 2359304 | tf_op jit(solution)/shard_map/ppermute | solution.py:22
  9.7 24.1 %collective-permute-start.2 = (bf16[3,256,512]{2,1,0:T(8,128)(2,1)S(1)}, bf16[3,256,512]{2,1,0:T(8,128)(2,1)S(1)}, u32[]{:S(2)}, u32[]{:S(2)}) collective-permute-start(bf16[3,256,512]{2,1,0:T(8,128)(2,1)S(1)} %get-tuple-element.21), channel_id=1, source_target_pairs={{0,31},{1,0},{2,1},{3,2},{4,3},{5,4},{6,5},{7,6},{8,7},{9,8},{10,9... | collective-permute-start | bytes 2359304 | tf_op jit(solution)/shard_map/ppermute | solution.py:22
  21.4 0.6 copy-start.9
  33.8 0.9 copy-start.2
  33.8 1.2 %copy-start.3 = (bf16[3,256,512]{2,1,0:T(8,128)(2,1)}, bf16[3,256,512]{2,1,0:T(8,128)(2,1)S(1)}, u32[]{:S(2)}) copy-start(bf16[3,256,512]{2,1,0:T(8,128)(2,1)S(1)} %collective-permute-done.2.refs_4_) | copy-start | bytes 2359300
  44.3 15.4 %collective-permute-start.3 = (f32[8,512]{1,0:T(8,128)}, f32[8,512]{1,0:T(8,128)S(1)}, u32[]{:S(2)}, u32[]{:S(2)}) collective-permute-start(f32[8,512]{1,0:T(8,128)} %get-tuple-element.23.refs_5_), channel_id=1, source_target_pairs={{0,31},{1,0},{2,1},{3,2},{4,3},{5,4},{6,5},{7,6},{8,7},{9,8},{10,9... | collective-permute-start | bytes 49160 | tf_op jit(solution)/shard_map/ppermute | solution.py:22
  47.8 11.9 %collective-permute-start.4 = (f32[8,512]{1,0:T(8,128)}, f32[8,512]{1,0:T(8,128)S(1)}, u32[]{:S(2)}, u32[]{:S(2)}) collective-permute-start(f32[8,512]{1,0:T(8,128)} %get-tuple-element.22.refs_2_), channel_id=1, source_target_pairs={{0,1},{1,2},{2,3},{3,4},{4,5},{5,6},{6,7},{7,8},{8,9},{9,10},{10,1... | collective-permute-start | bytes 49160 | tf_op jit(solution)/shard_map/ppermute | solution.py:22
  47.8 24.9 %collective-permute-start.5 = (bf16[3,256,512]{2,1,0:T(8,128)(2,1)}, bf16[3,256,512]{2,1,0:T(8,128)(2,1)S(1)}, u32[]{:S(2)}, u32[]{:S(2)}) collective-permute-start(bf16[3,256,512]{2,1,0:T(8,128)(2,1)} %get-tuple-element.27), channel_id=1, source_target_pairs={{0,1},{1,2},{2,3},{3,4},{4,5},{5,6},{6,7},{7,8},{8,9},{9,10},{10,1... | collective-permute-start | bytes 2359304 | tf_op jit(solution)/shard_map/ppermute | solution.py:22
  47.8 24.9 %collective-permute-start.6 = (bf16[3,256,512]{2,1,0:T(8,128)(2,1)}, bf16[3,256,512]{2,1,0:T(8,128)(2,1)S(1)}, u32[]{:S(2)}, u32[]{:S(2)}) collective-permute-start(bf16[3,256,512]{2,1,0:T(8,128)(2,1)} %get-tuple-element.28), channel_id=1, source_target_pairs={{0,31},{1,0},{2,1},{3,2},{4,3},{5,4},{6,5},{7,6},{8,7},{9,8},{10,9... | collective-permute-start | bytes 2359304 | tf_op jit(solution)/shard_map/ppermute | solution.py:22
  59.7 0.6 copy-start.7
  60.3 0.6 copy-start.10
  72.7 0.9 copy-start
  72.7 1.1 %copy-start.1 = (bf16[3,256,512]{2,1,0:T(8,128)(2,1)}, bf16[3,256,512]{2,1,0:T(8,128)(2,1)S(1)}, u32[]{:S(2)}) copy-start(bf16[3,256,512]{2,1,0:T(8,128)(2,1)S(1)} %collective-permute-done.6.refs_4_) | copy-start | bytes 2359300
  73.9 15.8 %copy-start.4 = (f32[3,512]{1,0:T(4,128)S(1)}, f32[3,512]{1,0:T(4,128)}, u32[]{:S(2)}) copy-start(f32[3,512]{1,0:T(4,128)} %param.7) | copy-start | bytes 18436
  73.9 15.8 %copy-start.6 = (f32[8,512]{1,0:T(8,128)S(1)}, f32[8,512]{1,0:T(8,128)}, u32[]{:S(2)}) copy-start(f32[8,512]{1,0:T(8,128)} %get-tuple-element.22.refs_2_) | copy-start | bytes 49156
  73.9 15.8 %copy-start.8 = (f32[8,512]{1,0:T(8,128)S(1)}, f32[8,512]{1,0:T(8,128)}, u32[]{:S(2)}) copy-start(f32[8,512]{1,0:T(8,128)} %copy-done.7) | copy-start | bytes 49156
  83.2 6.5 %collective-permute-start.7 = (f32[8,512]{1,0:T(8,128)}, f32[8,512]{1,0:T(8,128)S(1)}, u32[]{:S(2)}, u32[]{:S(2)}) collective-permute-start(f32[8,512]{1,0:T(8,128)} %get-tuple-element.31), channel_id=1, source_target_pairs={{0,31},{1,0},{2,1},{3,2},{4,3},{5,4},{6,5},{7,6},{8,7},{9,8},{10,9... | collective-permute-start | bytes 49160 | tf_op jit(solution)/shard_map/ppermute | solution.py:22
where the time goes:
time: 92.7 us; the launch traced here: 91 us
  Pallas kernels  64.5 us (70%)
  starting transfers between devices  12.7 us (14%)
  local copies, waits for them, and re-layouts  7.74 us (8%)
  other arithmetic  3.43 us (4%)
  between operations  1.47 us (2%)
  waiting for transfers between devices  1.06 us (1%)
    pallas_call x2, Pallas kernels, add_forcing(): pl.pallas_call(functools.partial(spread_kernel, layers, len(moved)), out_...  23.5 us
    pallas_call x2, Pallas kernels, stencil_terms(): pl.pallas_call(stencil_kernel, out_shape=jax.ShapeDtypeStruct(velocity.sh...  22.5 us
    pallas_call x2, Pallas kernels, finish_and_sample(): pl.pallas_call(functools.partial(sample_kernel, layers, send), out_shape=...  18.5 us
    ppermute x8, starting transfers between devices, shifted(): return lax.ppermute(value, 'gz', pairs)  12.7 us
    unnamed x22, local copies, waits for them, and re-layouts  4.1 us
    convert_element_type x1, local copies, waits for them, and re-layouts, local(): final = velocity[:, layers - 1].astype(jnp.bfloat16)  2.08 us
  transfers between devices with their start and end apart: 8, of which 1 were waited for; matrix products, arithmetic and copies ran while one was open for 0% of the time, Pallas kernels for 51%

commit v1 on v0

v1 whole, which is shorter than its diff:
```python
import functools
import math

import jax
import jax.numpy as jnp
from jax import lax
from jax.experimental import pallas as pl
from jax.experimental.pallas import tpu as pltpu
from jax.sharding import PartitionSpec as P

BLK = 256
STEPS = 2
DT = 0.2
VISC = 0.3
LANES = 128
PAD = 8
CHUNKS = 8
MESH = pl.DeviceIdType.MESH


def weights_of(offsets):
    angle = (0.5 * math.pi) * offsets
    c, s = jnp.cos(angle), jnp.sin(angle)
    return [0.25 * (1.0 + c), 0.25 * (1.0 + s), 0.25 * (1.0 - c), 0.25 * (1.0 - s)]


def banded(across, cell, weights, extent):
    apart = across - cell
    if extent & (extent - 1) == 0:
        apart = apart & (extent - 1)
    else:
        apart = jnp.where(apart < 0, apart + extent, apart)
    table = jnp.where(apart == 3, weights[3], 0.0)
    for j in (2, 1, 0):
        table = jnp.where(apart == j, weights[j], table)
    return table


def plane_weights(level, weights_z, layers):
    planes = []
    for z in range(layers):
        row = jnp.zeros(level.shape, jnp.float32)
        for j in range(4):
            row = jnp.where(level + j == z, weights_z[j], row)
        planes.append(row)
    return planes


def columns_of(rows):
    pad = -len(rows) % 8
    zero = jnp.zeros_like(rows[0])
    return jnp.concatenate(rows + [zero] * pad, axis=0).T


def kernel(
    v_hbm, off_ref, base_ref, tgt_ref, stiff_ref, cnt_ref,
    out_ref, offout_ref,
    vv, own, near, send, halo, low, lhs, xtab, xtab32, ytab, slhs, col, rowg, acc,
    partbuf, partin, in_sem, mk_sem, hs_sem, hr_sem, ps_sem, pr_sem,
):
    _, _, layers, nxb, nyp, _ = vv.shape
    ny = nyp - 2 * PAD
    nx = nxb * LANES
    markers = off_ref.shape[1]
    both = 2 * markers
    rows = ny // CHUNKS
    me = lax.axis_index("gz")
    count = lax.axis_size("gz")
    right = lax.rem(me + 1, count)
    left = lax.rem(me + count - 1, count)
    edges = (0, layers - 1)
    inner = tuple(range(1, layers - 1))
    order = inner + edges
    place = {z: i for i, z in enumerate(order)}

    barrier = pltpu.get_barrier_semaphore()
    for neighbour in (left, right):
        pl.semaphore_signal(barrier, inc=1, device_id=(neighbour,), device_id_type=MESH)

    def load(z, b):
        return pltpu.make_async_copy(
            v_hbm.at[:, z, :, pl.ds(b * LANES, LANES)],
            vv.at[0, :, z, b, pl.ds(PAD, ny), :],
            in_sem.at[z, b],
        )

    for z in edges + inner:
        for b in range(nxb):
            load(z, b).start()

    living = (
        lax.broadcasted_iota(jnp.int32, (1, markers), 1) // BLK < cnt_ref[0]
    ).astype(jnp.float32)
    own[0:3, :] = off_ref[...]
    own[3:5, :] = base_ref[0:2, :].astype(jnp.float32)
    own[5:6, :] = (base_ref[2:3, :] - me * layers).astype(jnp.float32)
    own[6:9, :] = tgt_ref[...]
    own[9:10, :] = living
    own[10:11, :] = living * stiff_ref[...]
    own[11:16, :] = jnp.zeros((5, markers), jnp.float32)

    pl.semaphore_wait(barrier, 2)
    marker_copy = pltpu.make_async_remote_copy(
        own, near, mk_sem.at[0], mk_sem.at[1], device_id=(right,), device_id_type=MESH
    )
    marker_copy.start()

    def halo_copy(step, side, k):
        r = pl.ds(k * rows, rows)
        if step == 0:
            source = send.at[side, :, r]
        else:
            source = low.at[:, pl.ds(place[edges[side]] * ny + k * rows, rows)]
        return pltpu.make_async_remote_copy(
            source,
            halo.at[step, 1 - side, :, r],
            hs_sem.at[step, side, k],
            hr_sem.at[step, 1 - side, k],
            device_id=((left, right)[side],),
            device_id_type=MESH,
        )

    for z in edges:
        for b in range(nxb):
            load(z, b).wait()

    def cast_chunk(k, _):
        for side, z in enumerate(edges):
            for c in range(3):
                for b in range(nxb):
                    send[side, c, pl.ds(k * rows, rows), b * LANES : (b + 1) * LANES] = vv[
                        0, c, z, b, pl.ds(PAD + k * rows, rows), :
                    ].astype(jnp.bfloat16)
        for side in range(2):
            halo_copy(0, side, k).start()
        return 0

    lax.fori_loop(0, CHUNKS, cast_chunk, 0)
    for z in inner:
        for b in range(nxb):
            load(z, b).wait()

    def wrap_rows(now):
        for c in range(3):
            for z in range(layers):
                for b in range(nxb):
                    vv[now, c, z, b, PAD - 1 : PAD, :] = vv[now, c, z, b, PAD + ny - 1 : PAD + ny, :]
                    vv[now, c, z, b, PAD + ny : PAD + ny + 1, :] = vv[now, c, z, b, PAD : PAD + 1, :]

    def stencil(now, z, n=8, unroll=2):
        lane = lax.broadcasted_iota(jnp.int32, (n, LANES), 1)
        first, last = lane == 0, lane == LANES - 1
        new = 1 - now

        def body(i, _):
            y0 = PAD + i * n
            here = [[vv[now, c, z, b, pl.ds(y0, n), :] for b in range(nxb)] for c in range(3)]
            fore = [[pltpu.roll(h, LANES - 1, 1) for h in hs] for hs in here]
            back = [[pltpu.roll(h, 1, 1) for h in hs] for hs in here]
            for b in range(nxb):
                up = [DT * VISC - (0.5 * DT) * here[c][b] for c in range(3)]
                down = [DT * VISC + (0.5 * DT) * here[c][b] for c in range(3)]
                for c in range(3):
                    total = (1.0 - 6.0 * DT * VISC) * here[c][b]
                    total += up[1] * vv[now, c, z, b, pl.ds(y0 + 1, n), :]
                    total += down[1] * vv[now, c, z, b, pl.ds(y0 - 1, n), :]
                    if z < layers - 1:
                        total += up[2] * vv[now, c, z + 1, b, pl.ds(y0, n), :]
                    if z > 0:
                        total += down[2] * vv[now, c, z - 1, b, pl.ds(y0, n), :]
                    total += up[0] * jnp.where(last, fore[c][(b + 1) % nxb], fore[c][b])
                    total += down[0] * jnp.where(first, back[c][(b - 1) % nxb], back[c][b])
                    vv[new, c, z, b, pl.ds(y0, n), :] = total
            return 0

        lax.fori_loop(0, ny // n, body, 0, unroll=unroll)

    def tables(step):
        halves = []
        for i, ref in enumerate((own, near)):
            info = ref[...]
            offsets = info[0:3]
            if step > 0:
                if i == 0:
                    moved = partbuf[step - 1, 0, 0:3, :] + partin[step - 1, 1, 0:3, :]
                else:
                    moved = partin[step - 1, 0, 0:3, :] + partbuf[step - 1, 1, 0:3, :]
                offsets = offsets + DT * (info[9:10] * moved)
                ref[0:3, :] = offsets
            level = info[5:6] - float(i * layers)
            forces = info[10:11] * (info[6:9] - offsets)
            halves.append((offsets, info[3:5].astype(jnp.int32), level.astype(jnp.int32), forces))
        offsets, cells, level, forces = [jnp.concatenate(p, axis=1) for p in zip(*halves)]
        weights = weights_of(offsets)
        planes = plane_weights(level, [w[2:3] for w in weights], layers)
        lines = []
        for a in range(2):
            lines += [cells[a : a + 1].astype(jnp.float32)] + [w[a : a + 1] for w in weights]
        col[...] = columns_of(lines + planes)
        for z in range(layers):
            for c in range(3):
                rowg[z, c : c + 1, :] = forces[c : c + 1] * planes[z]
        wy = [w[1:2] for w in weights]

        def ybody(i, _):
            across = lax.broadcasted_iota(jnp.int32, (32, both), 0) + i * 32
            ytab[pl.ds(i * 32, 32), :] = banded(across, cells[1:2], wy, ny)
            return 0

        lax.fori_loop(0, ny // 32, ybody, 0)
        chunk = 64

        def xbody(i, _):
            r = pl.ds(i * chunk, chunk)
            cols = col[r, :]
            across = lax.broadcasted_iota(jnp.int32, (chunk, nx), 1)
            cell = cols[:, 0:1].astype(jnp.int32)
            table = banded(across, cell, [cols[:, 1 + j : 2 + j] for j in range(4)], nx)
            xtab[r, :] = table.astype(jnp.bfloat16)
            xtab32[r, :] = table
            across = lax.broadcasted_iota(jnp.int32, (chunk, ny), 1)
            cell = cols[:, 5:6].astype(jnp.int32)
            y = banded(across, cell, [cols[:, 6 + j : 7 + j] for j in range(4)], ny)
            for z in range(layers):
                p = place[z] * ny
                slhs[r, p : p + ny] = (cols[:, 10 + z : 11 + z] * y).astype(jnp.bfloat16)
            return 0

        lax.fori_loop(0, both // chunk, xbody, 0)

    def spread(new, z):
        def lhs_body(i, _):
            y = ytab[pl.ds(i * 16, 16), :]
            for c in range(3):
                lhs[pl.ds(c * ny + i * 16, 16), :] = (rowg[z, c : c + 1, :] * y).astype(jnp.bfloat16)
            return 0

        lax.fori_loop(0, ny // 16, lhs_body, 0)
        force = jnp.dot(lhs[...], xtab[...], preferred_element_type=jnp.float32)
        for c in range(3):
            for b in range(nxb):
                vv[new, c, z, b, PAD : PAD + ny, :] += (
                    DT * force[c * ny : (c + 1) * ny, b * LANES : (b + 1) * LANES]
                )

    def lower_inner(new, final):
        def body(i, _):
            r = pl.ds(PAD + i * 16, 16)
            for z in inner:
                for c in range(3):
                    for b in range(nxb):
                        value = vv[new, c, z, b, r, :]
                        cut = slice(b * LANES, (b + 1) * LANES)
                        low[c, pl.ds(place[z] * ny + i * 16, 16), cut] = value.astype(jnp.bfloat16)
                        if final:
                            out_ref[c, z, pl.ds(i * 16, 16), cut] = value
            return 0

        lax.fori_loop(0, ny // 16, body, 0)

    def finish_edges(step, final, lo, hi):
        now, new = step % 2, 1 - step % 2

        def body(k, _):
            for side in range(2):
                halo_copy(step, 1 - side, k).wait_recv()
            for side, z in enumerate(edges):
                sign = (0.5 * DT, -0.5 * DT)[side]
                if final:
                    halo_copy(step, side, k).wait_send()
                for i in range(rows // 16):
                    y0 = k * rows + i * 16
                    for b in range(nxb):
                        cut = slice(b * LANES, (b + 1) * LANES)
                        factor = DT * VISC + sign * vv[now, 2, z, b, pl.ds(PAD + y0, 16), :]
                        for c in range(3):
                            value = vv[new, c, z, b, pl.ds(PAD + y0, 16), :] + factor * halo[
                                step, side, c, pl.ds(y0, 16), cut
                            ].astype(jnp.float32)
                            low[c, pl.ds(place[z] * ny + y0, 16), cut] = value.astype(jnp.bfloat16)
                            if final:
                                out_ref[c, z, pl.ds(y0, 16), cut] = value
                            else:
                                vv[new, c, z, b, pl.ds(PAD + y0, 16), :] = value
            if not final:
                for side in range(2):
                    halo_copy(step + 1, side, k).start()
            return 0

        lax.fori_loop(lo, hi, body, 0)

    def sample(first, final_part):
        depth = len(inner) * ny if first else len(edges) * ny
        base = 0 if first else len(inner) * ny

        def body(t, _):
            r = pl.ds(pl.multiple_of(t * 256, 256), 256)
            for c in range(3):
                lines = jnp.dot(
                    slhs[r, base : base + depth],
                    low[c, base : base + depth, :],
                    preferred_element_type=jnp.float32,
                )
                lines = lines * xtab32[r, :]
                total = lines[:, 0:LANES]
                for b in range(1, nxb):
                    total += lines[:, b * LANES : (b + 1) * LANES]
                if first:
                    acc[c, r, :] = total
                else:
                    acc[c, r, :] += total
            return 0

        lax.fori_loop(0, both // 256, body, 0)

    def parts(step):
        for part in range(2):
            r = slice(part * markers, (part + 1) * markers)
            sums = [jnp.sum(acc[c, r, :], axis=1, keepdims=True) for c in range(3)]
            zero = jnp.zeros((markers, 5), jnp.float32)
            partbuf[step, part] = jnp.concatenate(sums + [zero], axis=1).T

    def part_copy(step, part):
        return pltpu.make_async_remote_copy(
            partbuf.at[step, part],
            partin.at[step, part],
            ps_sem.at[step, part],
            pr_sem.at[step, part],
            device_id=((right, left)[part],),
            device_id_type=MESH,
        )

    for step in range(STEPS):
        now, new = step % 2, 1 - step % 2
        final = step == STEPS - 1
        wrap_rows(now)
        for z in edges + inner:
            stencil(now, z)
        if step == 0:
            marker_copy.wait()
        else:
            for part in range(2):
                part_copy(step - 1, part).wait()
        tables(step)
        for z in edges + inner:
            spread(new, z)
        finish_edges(step, final, 0, CHUNKS // 2)
        lower_inner(new, final)
        sample(True, False)
        finish_edges(step, final, CHUNKS // 2, CHUNKS)
        sample(False, final)
        parts(step)
        for part in range(1 if final else 0, 2):
            part_copy(step, part).start()
        if step == 0:
            for k in range(CHUNKS):
                for side in range(2):
                    halo_copy(0, side, k).wait_send()
    last = STEPS - 1
    part_copy(last, 1).wait()
    moved = partbuf[last, 0, 0:3, :] + partin[last, 1, 0:3, :]
    offout_ref[...] = own[0:3, :] + DT * (own[9:10, :] * moved)


def local(velocity, offsets, bases, targets, stiffness, active_block_count):
    _, layers, ny, nx = velocity.shape
    markers = offsets.shape[1]
    both = 2 * markers
    nxb = nx // LANES
    vmem = pl.BlockSpec(memory_space=pltpu.VMEM)
    hbm = pl.BlockSpec(memory_space=pl.ANY)
    smem = pl.BlockSpec(memory_space=pltpu.SMEM)
    f32, bf16 = jnp.float32, jnp.bfloat16
    dma = pltpu.SemaphoreType.DMA
    return pl.pallas_call(
        kernel,
        out_shape=[
            jax.ShapeDtypeStruct(velocity.shape, f32),
            jax.ShapeDtypeStruct(offsets.shape, f32),
        ],
        in_specs=[hbm, vmem, vmem, vmem, vmem, smem],
        out_specs=[vmem, vmem],
        scratch_shapes=[
            pltpu.VMEM((2, 3, layers, nxb, ny + 2 * PAD, LANES), f32),
            pltpu.VMEM((16, markers), f32),
            pltpu.VMEM((16, markers), f32),
            pltpu.VMEM((2, 3, ny, nx), bf16),
            pltpu.VMEM((STEPS, 2, 3, ny, nx), bf16),
            pltpu.VMEM((3, layers * ny, nx), bf16),
            pltpu.VMEM((3 * ny, both), bf16),
            pltpu.VMEM((both, nx), bf16),
            pltpu.VMEM((both, nx), f32),
            pltpu.VMEM((ny, both), f32),
            pltpu.VMEM((both, layers * ny), bf16),
            pltpu.VMEM((both, 16), f32),
            pltpu.VMEM((layers, 8, both), f32),
            pltpu.VMEM((3, both, LANES), f32),
            pltpu.VMEM((STEPS, 2, 8, markers), f32),
            pltpu.VMEM((STEPS, 2, 8, markers), f32),
            dma((layers, nxb)),
            dma((2,)),
            dma((STEPS, 2, CHUNKS)),
            dma((STEPS, 2, CHUNKS)),
            dma((STEPS, 2)),
            dma((STEPS, 2)),
        ],
        compiler_params=pltpu.CompilerParams(
            collective_id=0, has_side_effects=True, vmem_limit_bytes=60 * 1024 * 1024
        ),
        name="immersed_steps",
    )(velocity, offsets, bases, targets, stiffness.reshape(1, markers), active_block_count)


def solution(mesh):
    return jax.shard_map(
        local,
        mesh=mesh,
        in_specs=(
            P(None, "gz", None, None),
            P(None, "gz"),
            P(None, "gz"),
            P(None, "gz"),
            P("gz"),
            P("gz"),
        ),
        out_specs=(P(None, "gz", None, None), P(None, "gz")),
        check_vma=False,
    )
```

time: 92.7 us -> 70 us (0.76); the launches traced: 91 us -> 69.7 us
  starting transfers between devices: 12.7 us -> 0 us
  other arithmetic: 3.43 us -> 0 us
  Pallas kernels: 64.5 us -> 61.6 us
  waiting for transfers between devices: 1.06 us -> 0 us
  local copies, waits for them, and re-layouts: 7.74 us -> 6.8 us
    ppermute x8 -> x0, starting transfers between devices: 12.7 us -> none  [shifted(): return lax.ppermute(value, 'gz', pairs)]
    pallas_call x6 -> x1, Pallas kernels: 64.5 us -> 61.6 us  [local(): pl.pallas_call(kernel, out_shape=[jax.ShapeDtypeStruct(velocity.shape, f3...]
    unnamed x22 -> x4, local copies, waits for them, and re-layouts: 4.1 us -> 6.8 us
    convert_element_type x1 -> x0, local copies, waits for them, and re-layouts: 2.08 us -> none  [local(): final = velocity[:, layers - 1].astype(jnp.bfloat16)]
    concatenate x1 -> x0, local copies, waits for them, and re-layouts: 1.55 us -> none  [local(): jnp.concatenate([offsets, bases[:2].astype(jnp.float32), level[None].asty...]
    convert_element_type x4 -> x0, other arithmetic: 1.42 us -> none  [the longest x1 0.7 us: local(): level[None].astype(jnp.float32)]
    add x1 -> x0, other arithmetic: 1.33 us -> none  [local(): offsets = offsets + DT * (living[None, :] * (own_part[:3] + back[:3]))]
    ppermute x8 -> x0, waiting for transfers between devices: 1.06 us -> none  [shifted(): return lax.ppermute(value, 'gz', pairs)]
  transfers between devices with their start and end apart: 8 -> 0, of which waited for: 1 -> 0; matrix products, arithmetic and copies ran while one was open for 0% -> 0% of each run, Pallas kernels for 51% -> 0%
where the time goes in v1:
time: 70 us; the launch traced here: 69.7 us
  Pallas kernels  61.6 us (88%)
  local copies, waits for them, and re-layouts  6.8 us (10%)
  between operations  1.29 us (2%)
    pallas_call x1, Pallas kernels, local(): pl.pallas_call(kernel, out_shape=[jax.ShapeDtypeStruct(velocity.shape, f3...  61.6 us
    unnamed x4, local copies, waits for them, and re-layouts  6.8 us

profile of v1, /device:TPU:1, one launch (start us, length us, event | category | flops | bytes accessed | tf_op | source)
XLA Modules:
  0.0 69.7 jit_solution(4846998902175266827)
XLA Ops:
  1.3 61.6 %immersed_steps.1 = (f32[3,4,256,512]{3,2,1,0:T(8,128)}, f32[3,512]{1,0:T(4,128)}) custom-call(f32[3,4,256,512]{3,2,1,0:T(8,128)} %v_hbm.1, f32[3,512]{1,0:T(4,128)} %off_ref.1, s32[3,512]{1,0:T(4,128)} %base_ref.1, f32[3,512]{1,0:T(4,128)} %tgt_ref.1, f32[1,512]{1,0:T(1,128)} %bitcast.1, s32[1]{0:T(128)S(6)} %copy.10.cnt_ref), custom_call_target="tpu_custom_call" | custom-call | tf_op jit(solution)/shard_map/immersed_steps/pallas_call | solution.py:375
  62.9 0.0 copy-start
  62.9 6.2 %copy.11 = f32[3,4,256,512]{3,2,1,0:T(8,128)} copy(f32[3,4,256,512]{3,2,1,0:T(8,128)} %get-tuple-element.4) | data formatting | bytes 12582912
  69.1 0.0 copy-done
  69.1 0.6 copy.12
Async XLA Ops:
  62.9 6.2 %copy-start = (f32[3,512]{1,0:T(4,128)S(1)}, f32[3,512]{1,0:T(4,128)}, u32[]{:S(2)}) copy-start(f32[3,512]{1,0:T(4,128)} %get-tuple-element.5) | copy-start | bytes 18436

commit v2 on v1

v2 whole, which is shorter than its diff:
```python
import functools
import math

import jax
import jax.numpy as jnp
from jax import lax
from jax.experimental import pallas as pl
from jax.experimental.pallas import tpu as pltpu
from jax.sharding import PartitionSpec as P

BLK = 256
STEPS = 2
DT = 0.2
VISC = 0.3
LANES = 128
PAD = 8
CHUNKS = 8
STRIP = 32
EARLY = 2
MESH = pl.DeviceIdType.MESH


def weights_of(offsets):
    angle = (0.5 * math.pi) * offsets
    c, s = jnp.cos(angle), jnp.sin(angle)
    return [0.25 * (1.0 + c), 0.25 * (1.0 + s), 0.25 * (1.0 - c), 0.25 * (1.0 - s)]


def banded(across, cell, weights, extent):
    apart = across - cell
    if extent & (extent - 1) == 0:
        apart = apart & (extent - 1)
    else:
        apart = jnp.where(apart < 0, apart + extent, apart)
    table = jnp.where(apart == 3, weights[3], 0.0)
    for j in (2, 1, 0):
        table = jnp.where(apart == j, weights[j], table)
    return table


def plane_weights(level, weights_z, layers):
    planes = []
    for z in range(layers):
        row = jnp.zeros(level.shape, jnp.float32)
        for j in range(4):
            row = jnp.where(level + j == z, weights_z[j], row)
        planes.append(row)
    return planes


def kernel(
    v_hbm, off_hbm, base_hbm, tgt_hbm, stiff_hbm, cnt_ref,
    out_ref, corr_ref, elhs_ref, xown_ref, marks_ref,
    va, vb, ring, off_ref, base_ref, tgt_ref, stiff_ref, own, near, send, halo, lowt, lhs, xtab, xtab32,
    ytab, slhs, rowg, wrow, irow, sums, partin, arg_sem, in_sem, mk_sem, hs_sem, hr_sem, ps_sem, pr_sem,
):
    _, layers, nxb, nyp, _ = va.shape
    vv = (va, vb)
    ny = nyp - 2 * PAD
    nx = nxb * LANES
    markers = own.shape[1]
    both = 2 * markers
    rows = ny // CHUNKS
    me = lax.axis_index("gz")
    count = lax.axis_size("gz")
    right = lax.rem(me + 1, count)
    left = lax.rem(me + count - 1, count)
    edges = (0, layers - 1)
    inner = tuple(range(1, layers - 1))
    order = inner + edges
    place = {z: i for i, z in enumerate(order)}

    barrier = pltpu.get_barrier_semaphore()
    for neighbour in (left, right):
        pl.semaphore_signal(barrier, inc=1, device_id=(neighbour,), device_id_type=MESH)

    args = [
        pltpu.make_async_copy(source, target, arg_sem.at[i])
        for i, (source, target) in enumerate(
            ((off_hbm, off_ref), (base_hbm, base_ref), (tgt_hbm, tgt_ref), (stiff_hbm, stiff_ref))
        )
    ]
    for copy in args:
        copy.start()

    def load(z, b):
        return pltpu.make_async_copy(
            v_hbm.at[:, z, :, pl.ds(b * LANES, LANES)],
            va.at[:, z, b, pl.ds(PAD, ny), :],
            in_sem.at[z, b],
        )

    for z in edges + inner:
        for b in range(nxb):
            load(z, b).start()

    for copy in args:
        copy.wait()
    living = (
        lax.broadcasted_iota(jnp.int32, (1, markers), 1) // BLK < cnt_ref[0]
    ).astype(jnp.float32)
    own[0:3, :] = off_ref[...]
    own[3:5, :] = base_ref[0:2, :].astype(jnp.float32)
    own[5:6, :] = (base_ref[2:3, :] - me * layers).astype(jnp.float32)
    own[6:9, :] = tgt_ref[...]
    own[9:10, :] = living
    own[10:11, :] = living * stiff_ref[...]
    own[11:16, :] = jnp.zeros((5, markers), jnp.float32)

    pl.semaphore_wait(barrier, 2)
    marker_copy = pltpu.make_async_remote_copy(
        own, near, mk_sem.at[0], mk_sem.at[1], device_id=(right,), device_id_type=MESH
    )
    marker_copy.start()

    def halo_copy(step, side, k):
        r = pl.ds(k * rows, rows)
        return pltpu.make_async_remote_copy(
            send.at[step, side, :, r],
            halo.at[step, 1 - side, :, r],
            hs_sem.at[step, side, k],
            hr_sem.at[step, 1 - side, k],
            device_id=((left, right)[side],),
            device_id_type=MESH,
        )

    for z in edges:
        for b in range(nxb):
            load(z, b).wait()

    def cast_chunk(k, _):
        for side, z in enumerate(edges):
            for c in range(3):
                for b in range(nxb):
                    send[0, side, c, pl.ds(k * rows, rows), b * LANES : (b + 1) * LANES] = va[
                        c, z, b, pl.ds(PAD + k * rows, rows), :
                    ].astype(jnp.bfloat16)
        for side in range(2):
            halo_copy(0, side, k).start()
        return 0

    lax.fori_loop(0, CHUNKS, cast_chunk, 0)
    for z in inner:
        for b in range(nxb):
            load(z, b).wait()

    def wrap_rows(v):
        for c in range(3):
            for z in range(layers):
                for b in range(nxb):
                    v[c, z, b, PAD - 1 : PAD, :] = v[c, z, b, PAD + ny - 1 : PAD + ny, :]
                    v[c, z, b, PAD + ny : PAD + ny + 1, :] = v[c, z, b, PAD : PAD + 1, :]

    def shift_block(old, z, y0):
        lane = lax.broadcasted_iota(jnp.int32, (8, LANES), 1)
        first, last = lane == 0, lane == LANES - 1
        for j in range(STRIP // 8):
            for c in range(3):
                here = [old[c, z, b, pl.ds(y0 + 8 * j, 8), :] for b in range(nxb)]
                fore = [pltpu.roll(h, LANES - 1, 1) for h in here]
                back = [pltpu.roll(h, 1, 1) for h in here]
                for b in range(nxb):
                    r = slice(8 * j, 8 * j + 8)
                    ring[0, c, b, r, :] = jnp.where(last, fore[(b + 1) % nxb], fore[b])
                    ring[1, c, b, r, :] = jnp.where(first, back[(b - 1) % nxb], back[b])

    def stencil(old, new, z, after):
        steps = ny // STRIP

        def body(i, _):
            base = PAD + i * STRIP
            for j in range(STRIP // 8):
                y0 = base + 8 * j
                r = slice(8 * j, 8 * j + 8)
                for b in range(nxb):
                    here = [old[c, z, b, pl.ds(y0, 8), :] for c in range(3)]
                    half = [(0.5 * DT) * h for h in here]
                    up = [DT * VISC - h for h in half]
                    down = [DT * VISC + h for h in half]
                    for c in range(3):
                        total = (1.0 - 6.0 * DT * VISC) * here[c]
                        total += up[1] * old[c, z, b, pl.ds(y0 + 1, 8), :]
                        total += down[1] * old[c, z, b, pl.ds(y0 - 1, 8), :]
                        if z < layers - 1:
                            total += up[2] * old[c, z + 1, b, pl.ds(y0, 8), :]
                        if z > 0:
                            total += down[2] * old[c, z - 1, b, pl.ds(y0, 8), :]
                        total += up[0] * ring[0, c, b, r, :]
                        total += down[0] * ring[1, c, b, r, :]
                        new[c, z, b, pl.ds(y0, 8), :] = total
            done = i == steps - 1
            shift_block(old, jnp.where(done, after, z), jnp.where(done, PAD, base + STRIP))
            return 0

        lax.fori_loop(0, steps, body, 0)

    def tables(step, final):
        halves = []
        for i, ref in enumerate((own, near)):
            info = ref[...]
            offsets = info[0:3]
            if step > 0:
                if i == 0:
                    moved = sums[step - 1, 0, 0:3, :] + partin[step - 1, 1, 0:3, :]
                else:
                    moved = partin[step - 1, 0, 0:3, :] + sums[step - 1, 1, 0:3, :]
                offsets = offsets + DT * (info[9:10] * moved)
                ref[0:3, :] = offsets
            level = info[5:6] - float(i * layers)
            forces = info[10:11] * (info[6:9] - offsets)
            halves.append((offsets, info[3:5].astype(jnp.int32), level.astype(jnp.int32), forces))
        offsets, cells, level, forces = [jnp.concatenate(p, axis=1) for p in zip(*halves)]
        weights = weights_of(offsets)
        planes = plane_weights(level, [w[2:3] for w in weights], layers + 1)
        for z in range(layers):
            for c in range(3):
                rowg[z, c : c + 1, :] = forces[c : c + 1] * planes[z]
        irow[0:2, :] = cells[0:2]
        for a in range(2):
            for j in range(4):
                wrow[4 * a + j : 4 * a + j + 1, :] = weights[j][a : a + 1]
        for z in range(layers + 1):
            wrow[8 + z : 9 + z, :] = planes[z]
        tile, block = 256, 64

        def table_of(a, i, m, extent):
            across = lax.broadcasted_iota(jnp.int32, (block, tile), 0) + i * block
            w = [wrow[4 * a + j : 4 * a + j + 1, m] for j in range(4)]
            return banded(across, irow[a : a + 1, m], w, extent)

        for part in range(2):
            tiles = markers // tile

            def ybody(n, _):
                t, i = n % tiles, n // tiles
                r = pl.ds(pl.multiple_of(i * block, block), block)
                w = pl.ds(pl.multiple_of(t * tile, tile), tile)
                m = pl.ds(pl.multiple_of(part * markers + t * tile, tile), tile)
                table = table_of(1, i, m, ny)
                ytab[r, m] = table
                for z in range(layers):
                    if part == 1 and z > 2:
                        continue
                    plane = (wrow[8 + z : 9 + z, m] * table).astype(jnp.bfloat16)
                    slhs[pl.ds(place[z] * ny + i * block, block), m] = plane
                    if final and part == 0 and z in edges:
                        elhs_ref[pl.ds(edges.index(z) * ny + i * block, block), w] = plane
                if final and part == 0:
                    plane = wrow[8 + layers : 9 + layers, m] * table
                    elhs_ref[pl.ds(2 * ny + i * block, block), w] = plane.astype(jnp.bfloat16)
                return 0

            lax.fori_loop(0, tiles * (ny // block), ybody, 0)

            def xbody(n, _):
                t, i = n % tiles, n // tiles
                r = pl.ds(pl.multiple_of(i * block, block), block)
                w = pl.ds(pl.multiple_of(t * tile, tile), tile)
                m = pl.ds(pl.multiple_of(part * markers + t * tile, tile), tile)
                table = table_of(0, i, m, nx)
                xtab[r, m] = table.astype(jnp.bfloat16)
                xtab32[r, m] = table
                if final and part == 0:
                    xown_ref[r, w] = table
                return 0

            lax.fori_loop(0, tiles * (nx // block), xbody, 0)

    def spread(new, z, final):
        reach = both if z <= 2 else markers

        def lhs_body(i, _):
            y = ytab[pl.ds(i * 16, 16), :reach]
            for c in range(3):
                product = rowg[z, c : c + 1, :reach] * y
                lhs[pl.ds(c * ny + i * 16, 16), :reach] = product.astype(jnp.bfloat16)
            return 0

        lax.fori_loop(0, ny // 16, lhs_body, 0)
        force = lax.dot_general(
            lhs[:, :reach], xtab[:, :reach], (((1,), (1,)), ((), ())), preferred_element_type=jnp.float32
        )
        for c in range(3):
            for b in range(nxb):
                cut = slice(b * LANES, (b + 1) * LANES)
                value = new[c, z, b, PAD : PAD + ny, :] + DT * force[c * ny : (c + 1) * ny, cut]
                if final and z in inner:
                    out_ref[c, z, :, cut] = value
                else:
                    new[c, z, b, PAD : PAD + ny, :] = value

    def lower(new, planes, final):
        def body(c, _):
            for z in planes:
                for b in range(nxb):
                    cut = slice(b * LANES, (b + 1) * LANES)
                    if final and z in inner:
                        value = out_ref[c, z, :, cut]
                    else:
                        value = new[c, z, b, PAD : PAD + ny, :]
                    lowt[c, cut, place[z] * ny : (place[z] + 1) * ny] = value.astype(jnp.bfloat16).T
            return 0

        lax.fori_loop(0, 3, body, 0)

    def finish_edges(step, final, lo, hi, post=False):
        old, new = vv[step % 2], vv[1 - step % 2]
        cell = DT * VISC

        def body(k, _):
            for side in range(2):
                halo_copy(step, 1 - side, k).wait_recv()
            for i in range(rows // 16):
                y0 = k * rows + i * 16
                r = pl.ds(y0, 16)
                v = pl.ds(PAD + y0, 16)
                for b in range(nxb):
                    cut = slice(b * LANES, (b + 1) * LANES)
                    for side, z in enumerate(edges):
                        sign = (0.5 * DT, -0.5 * DT)[side]
                        outer = [halo[step, side, c, r, cut].astype(jnp.float32) for c in range(3)]
                        factor = cell + sign * old[2, z, b, v, :]
                        for c in range(3):
                            change = factor * outer[c]
                            value = new[c, z, b, v, :] + change
                            if final:
                                out_ref[c, z, r, cut] = value
                                corr_ref[side, c, r, cut] = change.astype(jnp.bfloat16)
                            else:
                                new[c, z, b, v, :] = value
                                send[step + 1, side, c, r, cut] = value.astype(jnp.bfloat16)
                        if final and side == 1:
                            beyond = cell + (0.5 * DT) * outer[2]
                            for c in range(3):
                                corr_ref[2, c, r, cut] = (beyond * old[c, z, b, v, :]).astype(jnp.bfloat16)
            if post:
                post_chunk(step + 1, k)
            return 0

        lax.fori_loop(lo, hi, body, 0)

    def post_chunk(step, k):
        for side in range(2):
            halo_copy(step, side, k).start()

    def sample(step, planes, first):
        base = place[planes[0]] * ny
        tile = 256

        for part in range(2):
            depth = len([z for z in planes if part == 0 or z <= 2]) * ny

            def body(t, _):
                m = pl.ds(pl.multiple_of(part * markers + t * tile, tile), tile)
                w = pl.ds(pl.multiple_of(t * tile, tile), tile)
                for c in range(3):
                    lines = jnp.dot(
                        lowt[c, :, base : base + depth],
                        slhs[base : base + depth, m],
                        preferred_element_type=jnp.float32,
                    )
                    total = jnp.sum(lines * xtab32[:, m], axis=0, keepdims=True)
                    if first:
                        sums[step, part, c : c + 1, w] = total
                    else:
                        sums[step, part, c : c + 1, w] += total
                return 0

            lax.fori_loop(0, markers // tile, body, 0)

    def part_copy(step, part):
        return pltpu.make_async_remote_copy(
            sums.at[step, part],
            partin.at[step, part],
            ps_sem.at[step, part],
            pr_sem.at[step, part],
            device_id=((right, left)[part],),
            device_id_type=MESH,
        )

    sums[...] = jnp.zeros_like(sums)
    for step in range(STEPS):
        old, new = vv[step % 2], vv[1 - step % 2]
        final = step == STEPS - 1
        wrap_rows(old)
        sweep = edges + inner
        shift_block(old, sweep[0], PAD)

        def stencils(planes):
            for z in planes:
                i = sweep.index(z)
                stencil(old, new, z, sweep[(i + 1) % layers])

        stencils(edges)
        if step == 0:
            marker_copy.wait()
        else:
            stencils(inner)
            for part in range(2):
                part_copy(step - 1, part).wait()
        tables(step, final)
        for z in edges:
            spread(new, z, final)
        if final:
            for z in inner:
                spread(new, z, final)
            lower(new, order, True)
            sample(step, order, True)
            part_copy(step, 1).start()
            finish_edges(step, True, 0, CHUNKS)
        else:
            finish_edges(step, False, 0, EARLY, True)
            stencils(inner)
            for z in inner:
                spread(new, z, final)
            lower(new, inner, False)
            sample(step, inner, True)
            finish_edges(step, False, EARLY, CHUNKS)
            lower(new, edges, False)
            sample(step, edges, False)
            for part in range(2):
                part_copy(step, part).start()
            for k in range(EARLY, CHUNKS):
                post_chunk(step + 1, k)
    last = STEPS - 1
    part_copy(last, 1).wait()
    marks_ref[0:3, :] = own[0:3, :]
    marks_ref[3:6, :] = sums[last, 0, 0:3, :] + partin[last, 1, 0:3, :]
    marks_ref[6:7, :] = own[9:10, :]
    marks_ref[7:8, :] = jnp.zeros((1, markers), jnp.float32)
    for step in range(STEPS):
        for k in range(CHUNKS):
            for side in range(2):
                halo_copy(step, side, k).wait_send()


def closing_kernel(v_ref, corr_ref, elhs_ref, x_ref, marks_ref, v_hbm, off_ref, cornt, sem):
    comps, layers, ny, nx = v_ref.shape
    copies = []
    for z in range(layers):
        for c in range(comps):
            copies.append(pltpu.make_async_copy(v_ref.at[c, z], v_hbm.at[c, z], sem.at[c, z]))
    for copy in copies:
        copy.start()
    for c in range(comps):
        for p in range(corr_ref.shape[0]):
            for b in range(nx // LANES):
                cut = slice(b * LANES, (b + 1) * LANES)
                cornt[c, cut, p * ny : (p + 1) * ny] = corr_ref[p, c, :, cut].T
        lines = jnp.dot(cornt[c], elhs_ref[...], preferred_element_type=jnp.float32)
        total = jnp.sum(lines * x_ref[...], axis=0, keepdims=True)
        off_ref[c : c + 1, :] = marks_ref[c : c + 1, :] + DT * (
            marks_ref[6:7, :] * (marks_ref[3 + c : 4 + c, :] + total)
        )
    for copy in copies:
        copy.wait()


def local(velocity, offsets, bases, targets, stiffness, active_block_count):
    _, layers, ny, nx = velocity.shape
    markers = offsets.shape[1]
    both = 2 * markers
    nxb = nx // LANES
    vmem = pl.BlockSpec(memory_space=pltpu.VMEM)
    hbm = pl.BlockSpec(memory_space=pl.ANY)
    smem = pl.BlockSpec(memory_space=pltpu.SMEM)
    f32, bf16 = jnp.float32, jnp.bfloat16
    dma = pltpu.SemaphoreType.DMA
    field = pltpu.VMEM((3, layers, nxb, ny + 2 * PAD, LANES), f32)
    results = pl.pallas_call(
        kernel,
        out_shape=[
            jax.ShapeDtypeStruct(velocity.shape, f32),
            jax.ShapeDtypeStruct((3, 3, ny, nx), bf16),
            jax.ShapeDtypeStruct((3 * ny, markers), bf16),
            jax.ShapeDtypeStruct((nx, markers), f32),
            jax.ShapeDtypeStruct((8, markers), f32),
        ],
        in_specs=[pl.BlockSpec(memory_space=pltpu.HBM)] * 5 + [smem],
        out_specs=[vmem] * 5,
        scratch_shapes=[
            field,
            field,
            pltpu.VMEM((2, 3, nxb, STRIP, LANES), f32),
            pltpu.VMEM((3, markers), f32),
            pltpu.VMEM((3, markers), jnp.int32),
            pltpu.VMEM((3, markers), f32),
            pltpu.VMEM((1, markers), f32),
            pltpu.VMEM((16, markers), f32),
            pltpu.VMEM((16, markers), f32),
            pltpu.VMEM((STEPS, 2, 3, ny, nx), bf16),
            pltpu.VMEM((STEPS, 2, 3, ny, nx), bf16),
            pltpu.VMEM((3, nx, layers * ny), bf16),
            pltpu.VMEM((3 * ny, both), bf16),
            pltpu.VMEM((nx, both), bf16),
            pltpu.VMEM((nx, both), f32),
            pltpu.VMEM((ny, both), f32),
            pltpu.VMEM((layers * ny, both), bf16),
            pltpu.VMEM((layers, 8, both), f32),
            pltpu.VMEM((16, both), f32),
            pltpu.VMEM((8, both), jnp.int32),
            pltpu.VMEM((STEPS, 2, 8, markers), f32),
            pltpu.VMEM((STEPS, 2, 8, markers), f32),
            dma((4,)),
            dma((layers, nxb)),
            dma((2,)),
            dma((STEPS, 2, CHUNKS)),
            dma((STEPS, 2, CHUNKS)),
            dma((STEPS, 2)),
            dma((STEPS, 2)),
        ],
        compiler_params=pltpu.CompilerParams(
            collective_id=0, has_side_effects=True, vmem_limit_bytes=40 * 1024 * 1024
        ),
        name="immersed_steps",
    )(
        velocity,
        *[
            pltpu.with_memory_space_constraint(a, pltpu.HBM)
            for a in (offsets, bases, targets, stiffness.reshape(1, markers))
        ],
        active_block_count,
    )
    return pl.pallas_call(
        closing_kernel,
        out_shape=[
            jax.ShapeDtypeStruct(velocity.shape, f32),
            jax.ShapeDtypeStruct(offsets.shape, f32),
        ],
        in_specs=[vmem] * 5,
        out_specs=[hbm, vmem],
        scratch_shapes=[pltpu.VMEM((3, nx, 3 * ny), bf16), dma((3, layers))],
        compiler_params=pltpu.CompilerParams(vmem_limit_bytes=16 * 1024 * 1024),
        name="closing",
    )(*results)


def solution(mesh):
    return jax.shard_map(
        local,
        mesh=mesh,
        in_specs=(
            P(None, "gz", None, None),
            P(None, "gz"),
            P(None, "gz"),
            P(None, "gz"),
            P("gz"),
            P("gz"),
        ),
        out_specs=(P(None, "gz", None, None), P(None, "gz")),
        check_vma=False,
    )
```

time: 70 us -> 55.8 us (0.80)
  Pallas kernels: 61.6 us -> 54.3 us
  local copies, waits for them, and re-layouts: 6.8 us -> 0 us
    pallas_call x1, Pallas kernels: 61.6 us -> 50.5 us  [local(): pl.pallas_call(kernel, out_shape=[jax.ShapeDtypeStruct(velocity.shape, f3...]
    unnamed x4 -> x0, local copies, waits for them, and re-layouts: 6.8 us -> none
    pallas_call x0 -> x1, Pallas kernels: none -> 3.77 us  [local(): pl.pallas_call(closing_kernel, out_shape=[jax.ShapeDtypeStruct(velocity.s...]
where the time goes in v2:
time: 55.8 us; the launch traced here: 55.5 us
  Pallas kernels  54.3 us (97%)
  between operations  1.29 us (2%)
    pallas_call x1, Pallas kernels, local(): pl.pallas_call(kernel, out_shape=[jax.ShapeDtypeStruct(velocity.shape, f3...  50.5 us
    pallas_call x1, Pallas kernels, local(): pl.pallas_call(closing_kernel, out_shape=[jax.ShapeDtypeStruct(velocity.s...  3.77 us

profile of v2, /device:TPU:1, one launch (start us, length us, event | category | flops | bytes accessed | tf_op | source)
XLA Modules:
  0.0 55.5 jit_solution(17742052578734210243)
XLA Ops:
  1.3 50.5 %immersed_steps.1 = (f32[3,4,256,512]{3,2,1,0:T(8,128)S(1)}, bf16[3,3,256,512]{3,2,1,0:T(8,128)(2,1)S(1)}, bf16[768,512]{1,0:T(8,128)(2,1)S(1)}, f32[512,512]{1,0:T(8,128)S(1)}, f32[8,512]{1,0:T(8,128)S(1)}) custom-call(f32[3,4,256,512]{3,2,1,0:T(8,128)} %v_hbm.1, f32[3,512]{1,0:T(4,128)} %off_hbm.1, s32[3,512]{1,0:T(4,128)} %base_hbm.1, f32[3,512]{1,0:T(4,128)} %tgt_hbm.1, ...), custom_call_target="tpu_custom_call" | custom-call | tf_op jit(solution)/shard_map/immersed_steps/pallas_call | solution.py:470
  51.8 3.8 %closing.1 = (f32[3,4,256,512]{3,2,1,0:T(8,128)}, f32[3,512]{1,0:T(4,128)}) custom-call(f32[3,4,256,512]{3,2,1,0:T(8,128)S(1)} %get-tuple-element.7.v_ref, bf16[3,3,256,512]{3,2,1,0:T(8,128)(2,1)S(1)} %get-tuple-element.8.corr_ref, bf16[768,512]{1,0:T(8,128)(2,1)S(1)} %get-tuple-element.9.elhs_ref, f32[512,512]{1,0:T(8,128)S(1)} %get-tuple-element.10.x_ref, ...), custom_call_target="tpu_custom_call" | custom-call | tf_op jit(solution)/shard_map/closing/pallas_call | solution.py:524
